TPU v7x, 512 devices: a whole 4x4x16 slice. The times are simulated.
512 devices in a mesh: cand: 64 (over z, x), env: 8 (over y, core).
Axes of the slice: x: 4, y: 4, z: 16, core: 2. Of those that a mesh axis runs over, the one named last changes fastest.
Arguments:
- plan_mean: float32 [512, 512], P(('env', 'cand')), parts along dimension 0, may hold values from -0.5 to 0.5
- plan_var: float32 [512, 512], P(('env', 'cand')), parts along dimension 0, may hold values from 0.04 to 0.64
- start_state: float32 [512, 128], P(('env', 'cand')), parts along dimension 0, may hold values from -6 to 6
- noise: bfloat16 [512, 512, 512], P('env', 'cand'), parts along dimension 0, may hold values from -6 to 6
- elite_index: int32 [512, 64], P('env'), parts along dimension 0, may hold values from 0 to 511, as said below
- w_state: bfloat16 [4, 128, 512], replicated, may hold values from -0.5 to 0.5
- w_act: bfloat16 [4, 32, 512], replicated, may hold values from -1 to 1
- bias_hidden: float32 [4, 512], replicated, may hold values from -3 to 3
- w_out: bfloat16 [4, 512, 128], replicated, may hold values from -0.125 to 0.125
Outputs:
- returns: float32 [512, 512], P('env', 'cand'), parts along dimension 0
- new_mean: float32 [512, 512], P(('env', 'cand')), parts along dimension 0
- new_var: float32 [512, 512], P(('env', 'cand')), parts along dimension 0
There are 8 independent parts, one for each index of `env`. A program takes and returns all parts, laid end to end along the dimension named above; an argument that names none is the same for every part. Nothing has to cross between parts.
Inputs may be any that keep to these rules, and one draw needn't show every extreme that they name: `elite_index`: row e lists 64 different candidates of environment e. Among the candidates 8 * b to 8 * (b + 1) - 1 of one environment at most 4 are listed, and in every environment some such block holds exactly 4.
All inputs are finite; a program needn't handle non-finite values.
Results may differ from a plain program's by a relative error of at most 0.0012.
Values may be sent and summed in bfloat16 or wider, within the bound.
A program may use at most 64 MiB of HBM per device.

v0:
```python
import jax
import jax.numpy as jnp
from jax import lax
from jax.sharding import PartitionSpec as P

ELITE = 64


ALPHA = 0.1
EPSILON = 1e-06


def in_one_piece(arrays, axis, dim, along):
    ends, at = ([], 0)
    for a in arrays[:-1]:
        at += a.shape[along]
        ends.append(at)
    both = jnp.concatenate(arrays, axis=along)
    return tuple(jnp.split(lax.all_gather(both, axis, axis=dim, tiled=True), ends, axis=along))


def in_blocks(value, dim, devices):
    lengths = value.shape
    pieces = value.reshape(*lengths[:dim], devices, lengths[dim] // devices, *lengths[dim + 1 :])
    return jnp.moveaxis(pieces, dim, 0)


def sent_and_summed(value, axis, dim):
    devices = lax.axis_size(axis)
    pieces = lax.all_to_all(in_blocks(value, dim, devices), axis, 0, 0, tiled=True)
    return jnp.sum(pieces, axis=0)


def in_one_piece_2(arrays, axis, dim, along):
    ends, at = ([], 0)
    for a in arrays[:-1]:
        at += a.shape[along]
        ends.append(at)
    both = jnp.concatenate(arrays, axis=along)
    return tuple(jnp.split(sent_and_summed(both, axis, dim), ends, axis=along))


def rollout(actions, start_state, w_state, w_act, bias_hidden, w_out):
    env_count = actions.shape[0]
    cand_count = actions.shape[1]
    members = w_state.shape[0]
    features = w_state.shape[1]
    act_width = w_act.shape[1]
    horizon = actions.shape[2] // act_width
    groups = cand_count // members
    states = jnp.broadcast_to(start_state[:, None, :], (env_count, cand_count, features))
    running = jnp.zeros((env_count, cand_count), jnp.float32)

    def advance(step_index, loop_state):
        states, running = loop_state
        step_act = lax.dynamic_slice_in_dim(actions, step_index * act_width, act_width, 2)
        energy = jnp.mean(states * states, axis=-1, keepdims=True) + EPSILON
        normed = (states * lax.rsqrt(energy)).astype(jnp.bfloat16)
        grouped = normed.reshape(env_count, groups, members, features)
        act_grouped = step_act.reshape(env_count, groups, members, act_width)
        preact = jnp.einsum("egms,msh->egmh", grouped, w_state, preferred_element_type=jnp.float32)
        preact = preact + jnp.einsum(
            "egma,mah->egmh", act_grouped, w_act, preferred_element_type=jnp.float32
        )
        preact = preact + bias_hidden[None, None, :, :]
        hidden = jax.nn.silu(preact).astype(jnp.bfloat16)
        change = jnp.einsum("egmh,mhs->egms", hidden, w_out, preferred_element_type=jnp.float32)
        states = states + change.reshape(env_count, cand_count, features)
        act_float = step_act.astype(jnp.float32)
        reward = -jnp.mean(states * states, axis=-1) - 0.1 * jnp.mean(
            act_float * act_float, axis=-1
        )
        return (states, running + reward)

    states, running = lax.fori_loop(0, horizon, advance, (states, running))
    return running / horizon


def per_device(
    plan_mean, plan_var, start_state, noise, elite_index, w_state, w_act, bias_hidden, w_out
):
    full_mean, full_var, full_start = in_one_piece((plan_mean, plan_var, start_state), "cand", 0, 1)
    actions = jnp.clip(
        full_mean[:, None, :] + jnp.sqrt(full_var)[:, None, :] * noise.astype(jnp.float32),
        -1.0,
        1.0,
    ).astype(jnp.bfloat16)
    returns = rollout(actions, full_start, w_state, w_act, bias_hidden, w_out)
    local_count = noise.shape[1]
    offset = lax.axis_index("cand") * local_count
    positions = offset + jnp.arange(local_count, dtype=jnp.int32)
    chosen = jnp.any(elite_index[:, :, None] == positions[None, None, :], axis=1)
    values = actions.astype(jnp.float32)
    picked = chosen.astype(jnp.float32)[:, :, None]
    first_sum, second_sum = in_one_piece_2(
        (jnp.sum(values * picked, axis=1), jnp.sum(values * values * picked, axis=1)), "cand", 0, 1
    )
    elite_mean = first_sum / ELITE
    elite_var = second_sum / ELITE - elite_mean * elite_mean
    new_mean = ALPHA * plan_mean + (1.0 - ALPHA) * elite_mean
    new_var = ALPHA * plan_var + (1.0 - ALPHA) * elite_var
    return (returns, new_mean, new_var)


def solution(mesh):
    in_specs = (
        P(("env", "cand"), None),
        P(("env", "cand"), None),
        P(("env", "cand"), None),
        P("env", "cand", None),
        P("env", None),
        P(),
        P(),
        P(),
        P(),
    )
    out_specs = (P("env", "cand"), P(("env", "cand"), None), P(("env", "cand"), None))
    return jax.shard_map(
        per_device, mesh=mesh, in_specs=in_specs, out_specs=out_specs, check_vma=False
    )
```

profile of v0, /device:TPU:24, one launch (start us, length us, event | category | flops | bytes accessed | tf_op | source)
XLA Modules:
  0.0 159.6 jit_solution(16418242446190204262)
XLA Ops:
  0.6 0.7 maximum_bitcast_fusion.1
  1.4 102.1 %all-gather = f32[64,1,1152]{2,1,0:T(1,128)S(1)} all-gather(f32[1,1,1152]{2,1,0:T(1,128)S(1)} %maximum_bitcast_fusion.1), channel_id=1, replica_groups=mesh['cand'=64,'env'=8] {'cand'}, dimensions={0}, use_global_device_ids=true | all-gather | bytes 299520 | tf_op jit(solution)/shard_map/all_gather | solution.py:19
  103.8 0.6 copy.45
  104.5 1.2 compare_reduce_fusion
  105.8 0.9 fusion.13
  106.8 0.9 copy.47
  107.7 9.9 %all-to-all-start = ((f32[64,1,1024]{2,1,0:T(1,128)}), f32[64,1,1024]{2,1,0:T(1,128)}, u32[]{:S(2)}, u32[]{:S(2)}) async-start(f32[64,1,1024]{2,1,0:T(1,128)} %copy.47), calls=%async_computation | async-start | bytes 524288 | tf_op jit(solution)/shard_map/all_to_all | solution.py:30
  117.7 0.1 broadcast_reduce_fusion
  117.9 39.4 %while.18 = (s32[]{:T(128)}, f32[64,8,128]{2,0,1:T(8,128)S(1)}, f32[64,8]{0,1:T(8,128)S(1)}, bf16[4,128,512]{2,1,0:T(8,128)(2,1)S(1)}, bf16[64,8,512]{0,2,1:T(8,...) while((s32[]{:T(128)}, f32[64,8,128]{2,0,1:T(8,128)S(1)}, ...), condition=%wide.region_4.5_spmd.clone, body=%wide.region_0.4_spmd.clone.sunk | while | flops 153209856 | bytes 5761209 | solution.py:75
  118.0 0.1 multiply_convert_fusion.3
  118.1 0.3 fusion.29
  118.4 1.7 %convolution_bitcast_fusion.2 = f32[64,2,4,128]{3,0,1,2:T(8,128)S(1)} fusion(f32[4,64,2,512]{3,1,2,0:T(8,128)S(1)} %fusion.29, bf16[4,512,128]{2,1,0:T(8,128)(2,1)} %get-tuple-element.391, f32[4,512]{1,0:T(4,128)S(1)} %get-tuple-element.390, bf16[4,32,512]{2,1,0:T(8,128)(2,1)S(1)} %get-tuple-element.389, bf16[64,2,4,32]{0,3,2,1:T(8,128)(2,1)S(1)} %bitcast.53), kind=kOutput, calls=%fused_computation.3.clone.1 | convolution fusion | flops 85721088 | bytes 2007040 | tf_op jit(solution)/shard_map/while/body/eval_jaxpr/egmh,mhs->egms/dot_general | solution.py:67
  120.2 0.1 multiply_reduce_fusion.5
  120.6 0.3 fusion.29
  120.9 1.7 %convolution_bitcast_fusion.2 = f32[64,2,4,128]{3,0,1,2:T(8,128)S(1)} fusion(f32[4,64,2,512]{3,1,2,0:T(8,128)S(1)} %fusion.29, bf16[4,512,128]{2,1,0:T(8,128)(2,1)} %get-tuple-element.391, f32[4,512]{1,0:T(4,128)S(1)} %get-tuple-element.390, bf16[4,32,512]{2,1,0:T(8,128)(2,1)S(1)} %get-tuple-element.389, bf16[64,2,4,32]{0,3,2,1:T(8,128)(2,1)S(1)} %bitcast.53), kind=kOutput, calls=%fused_computation.3.clone.1 | convolution fusion | flops 85721088 | bytes 2007040 | tf_op jit(solution)/shard_map/while/body/eval_jaxpr/egmh,mhs->egms/dot_general | solution.py:67
  122.7 0.1 multiply_reduce_fusion.5
  123.0 0.3 fusion.29
  123.3 1.7 %convolution_bitcast_fusion.2 = f32[64,2,4,128]{3,0,1,2:T(8,128)S(1)} fusion(f32[4,64,2,512]{3,1,2,0:T(8,128)S(1)} %fusion.29, bf16[4,512,128]{2,1,0:T(8,128)(2,1)} %get-tuple-element.391, f32[4,512]{1,0:T(4,128)S(1)} %get-tuple-element.390, bf16[4,32,512]{2,1,0:T(8,128)(2,1)S(1)} %get-tuple-element.389, bf16[64,2,4,32]{0,3,2,1:T(8,128)(2,1)S(1)} %bitcast.53), kind=kOutput, calls=%fused_computation.3.clone.1 | convolution fusion | flops 85721088 | bytes 2007040 | tf_op jit(solution)/shard_map/while/body/eval_jaxpr/egmh,mhs->egms/dot_general | solution.py:67
  125.1 0.1 multiply_reduce_fusion.5
  125.4 0.1 multiply_convert_fusion.3
  125.5 0.3 fusion.29
  125.8 1.7 %convolution_bitcast_fusion.2 = f32[64,2,4,128]{3,0,1,2:T(8,128)S(1)} fusion(f32[4,64,2,512]{3,1,2,0:T(8,128)S(1)} %fusion.29, bf16[4,512,128]{2,1,0:T(8,128)(2,1)} %get-tuple-element.391, f32[4,512]{1,0:T(4,128)S(1)} %get-tuple-element.390, bf16[4,32,512]{2,1,0:T(8,128)(2,1)S(1)} %get-tuple-element.389, bf16[64,2,4,32]{0,3,2,1:T(8,128)(2,1)S(1)} %bitcast.53), kind=kOutput, calls=%fused_computation.3.clone.1 | convolution fusion | flops 85721088 | bytes 2007040 | tf_op jit(solution)/shard_map/while/body/eval_jaxpr/egmh,mhs->egms/dot_general | solution.py:67
  127.6 0.1 multiply_reduce_fusion.5
  127.8 0.1 multiply_convert_fusion.3
  128.0 0.3 fusion.29
  128.3 1.7 %convolution_bitcast_fusion.2 = f32[64,2,4,128]{3,0,1,2:T(8,128)S(1)} fusion(f32[4,64,2,512]{3,1,2,0:T(8,128)S(1)} %fusion.29, bf16[4,512,128]{2,1,0:T(8,128)(2,1)} %get-tuple-element.391, f32[4,512]{1,0:T(4,128)S(1)} %get-tuple-element.390, bf16[4,32,512]{2,1,0:T(8,128)(2,1)S(1)} %get-tuple-element.389, bf16[64,2,4,32]{0,3,2,1:T(8,128)(2,1)S(1)} %bitcast.53), kind=kOutput, calls=%fused_computation.3.clone.1 | convolution fusion | flops 85721088 | bytes 2007040 | tf_op jit(solution)/shard_map/while/body/eval_jaxpr/egmh,mhs->egms/dot_general | solution.py:67
  130.1 0.1 multiply_reduce_fusion.5
  130.4 0.3 fusion.29
  130.7 1.7 %convolution_bitcast_fusion.2 = f32[64,2,4,128]{3,0,1,2:T(8,128)S(1)} fusion(f32[4,64,2,512]{3,1,2,0:T(8,128)S(1)} %fusion.29, bf16[4,512,128]{2,1,0:T(8,128)(2,1)} %get-tuple-element.391, f32[4,512]{1,0:T(4,128)S(1)} %get-tuple-element.390, bf16[4,32,512]{2,1,0:T(8,128)(2,1)S(1)} %get-tuple-element.389, bf16[64,2,4,32]{0,3,2,1:T(8,128)(2,1)S(1)} %bitcast.53), kind=kOutput, calls=%fused_computation.3.clone.1 | convolution fusion | flops 85721088 | bytes 2007040 | tf_op jit(solution)/shard_map/while/body/eval_jaxpr/egmh,mhs->egms/dot_general | solution.py:67
  132.5 0.1 multiply_reduce_fusion.5
  132.9 0.3 fusion.29
  133.2 1.7 %convolution_bitcast_fusion.2 = f32[64,2,4,128]{3,0,1,2:T(8,128)S(1)} fusion(f32[4,64,2,512]{3,1,2,0:T(8,128)S(1)} %fusion.29, bf16[4,512,128]{2,1,0:T(8,128)(2,1)} %get-tuple-element.391, f32[4,512]{1,0:T(4,128)S(1)} %get-tuple-element.390, bf16[4,32,512]{2,1,0:T(8,128)(2,1)S(1)} %get-tuple-element.389, bf16[64,2,4,32]{0,3,2,1:T(8,128)(2,1)S(1)} %bitcast.53), kind=kOutput, calls=%fused_computation.3.clone.1 | convolution fusion | flops 85721088 | bytes 2007040 | tf_op jit(solution)/shard_map/while/body/eval_jaxpr/egmh,mhs->egms/dot_general | solution.py:67
  135.0 0.1 multiply_reduce_fusion.5
  135.2 0.1 multiply_convert_fusion.3
  135.3 0.3 fusion.29
  135.6 1.7 %convolution_bitcast_fusion.2 = f32[64,2,4,128]{3,0,1,2:T(8,128)S(1)} fusion(f32[4,64,2,512]{3,1,2,0:T(8,128)S(1)} %fusion.29, bf16[4,512,128]{2,1,0:T(8,128)(2,1)} %get-tuple-element.391, f32[4,512]{1,0:T(4,128)S(1)} %get-tuple-element.390, bf16[4,32,512]{2,1,0:T(8,128)(2,1)S(1)} %get-tuple-element.389, bf16[64,2,4,32]{0,3,2,1:T(8,128)(2,1)S(1)} %bitcast.53), kind=kOutput, calls=%fused_computation.3.clone.1 | convolution fusion | flops 85721088 | bytes 2007040 | tf_op jit(solution)/shard_map/while/body/eval_jaxpr/egmh,mhs->egms/dot_general | solution.py:67
  137.4 0.1 multiply_reduce_fusion.5
  137.8 0.3 fusion.29
  138.1 1.7 %convolution_bitcast_fusion.2 = f32[64,2,4,128]{3,0,1,2:T(8,128)S(1)} fusion(f32[4,64,2,512]{3,1,2,0:T(8,128)S(1)} %fusion.29, bf16[4,512,128]{2,1,0:T(8,128)(2,1)} %get-tuple-element.391, f32[4,512]{1,0:T(4,128)S(1)} %get-tuple-element.390, bf16[4,32,512]{2,1,0:T(8,128)(2,1)S(1)} %get-tuple-element.389, bf16[64,2,4,32]{0,3,2,1:T(8,128)(2,1)S(1)} %bitcast.53), kind=kOutput, calls=%fused_computation.3.clone.1 | convolution fusion | flops 85721088 | bytes 2007040 | tf_op jit(solution)/shard_map/while/body/eval_jaxpr/egmh,mhs->egms/dot_general | solution.py:67
  139.9 0.1 multiply_reduce_fusion.5
  140.3 0.3 fusion.29
  140.6 1.7 %convolution_bitcast_fusion.2 = f32[64,2,4,128]{3,0,1,2:T(8,128)S(1)} fusion(f32[4,64,2,512]{3,1,2,0:T(8,128)S(1)} %fusion.29, bf16[4,512,128]{2,1,0:T(8,128)(2,1)} %get-tuple-element.391, f32[4,512]{1,0:T(4,128)S(1)} %get-tuple-element.390, bf16[4,32,512]{2,1,0:T(8,128)(2,1)S(1)} %get-tuple-element.389, bf16[64,2,4,32]{0,3,2,1:T(8,128)(2,1)S(1)} %bitcast.53), kind=kOutput, calls=%fused_computation.3.clone.1 | convolution fusion | flops 85721088 | bytes 2007040 | tf_op jit(solution)/shard_map/while/body/eval_jaxpr/egmh,mhs->egms/dot_general | solution.py:67
  142.4 0.1 multiply_reduce_fusion.5
  142.7 0.3 fusion.29
  143.0 1.7 %convolution_bitcast_fusion.2 = f32[64,2,4,128]{3,0,1,2:T(8,128)S(1)} fusion(f32[4,64,2,512]{3,1,2,0:T(8,128)S(1)} %fusion.29, bf16[4,512,128]{2,1,0:T(8,128)(2,1)} %get-tuple-element.391, f32[4,512]{1,0:T(4,128)S(1)} %get-tuple-element.390, bf16[4,32,512]{2,1,0:T(8,128)(2,1)S(1)} %get-tuple-element.389, bf16[64,2,4,32]{0,3,2,1:T(8,128)(2,1)S(1)} %bitcast.53), kind=kOutput, calls=%fused_computation.3.clone.1 | convolution fusion | flops 85721088 | bytes 2007040 | tf_op jit(solution)/shard_map/while/body/eval_jaxpr/egmh,mhs->egms/dot_general | solution.py:67
  144.8 0.1 multiply_reduce_fusion.5
  145.2 0.3 fusion.29
  145.5 1.7 %convolution_bitcast_fusion.2 = f32[64,2,4,128]{3,0,1,2:T(8,128)S(1)} fusion(f32[4,64,2,512]{3,1,2,0:T(8,128)S(1)} %fusion.29, bf16[4,512,128]{2,1,0:T(8,128)(2,1)} %get-tuple-element.391, f32[4,512]{1,0:T(4,128)S(1)} %get-tuple-element.390, bf16[4,32,512]{2,1,0:T(8,128)(2,1)S(1)} %get-tuple-element.389, bf16[64,2,4,32]{0,3,2,1:T(8,128)(2,1)S(1)} %bitcast.53), kind=kOutput, calls=%fused_computation.3.clone.1 | convolution fusion | flops 85721088 | bytes 2007040 | tf_op jit(solution)/shard_map/while/body/eval_jaxpr/egmh,mhs->egms/dot_general | solution.py:67
  147.3 0.1 multiply_reduce_fusion.5
  147.7 0.3 fusion.29
  147.9 1.7 %convolution_bitcast_fusion.2 = f32[64,2,4,128]{3,0,1,2:T(8,128)S(1)} fusion(f32[4,64,2,512]{3,1,2,0:T(8,128)S(1)} %fusion.29, bf16[4,512,128]{2,1,0:T(8,128)(2,1)} %get-tuple-element.391, f32[4,512]{1,0:T(4,128)S(1)} %get-tuple-element.390, bf16[4,32,512]{2,1,0:T(8,128)(2,1)S(1)} %get-tuple-element.389, bf16[64,2,4,32]{0,3,2,1:T(8,128)(2,1)S(1)} %bitcast.53), kind=kOutput, calls=%fused_computation.3.clone.1 | convolution fusion | flops 85721088 | bytes 2007040 | tf_op jit(solution)/shard_map/while/body/eval_jaxpr/egmh,mhs->egms/dot_general | solution.py:67
  149.7 0.1 multiply_reduce_fusion.5
  150.1 0.3 fusion.29
  150.4 1.7 %convolution_bitcast_fusion.2 = f32[64,2,4,128]{3,0,1,2:T(8,128)S(1)} fusion(f32[4,64,2,512]{3,1,2,0:T(8,128)S(1)} %fusion.29, bf16[4,512,128]{2,1,0:T(8,128)(2,1)} %get-tuple-element.391, f32[4,512]{1,0:T(4,128)S(1)} %get-tuple-element.390, bf16[4,32,512]{2,1,0:T(8,128)(2,1)S(1)} %get-tuple-element.389, bf16[64,2,4,32]{0,3,2,1:T(8,128)(2,1)S(1)} %bitcast.53), kind=kOutput, calls=%fused_computation.3.clone.1 | convolution fusion | flops 85721088 | bytes 2007040 | tf_op jit(solution)/shard_map/while/body/eval_jaxpr/egmh,mhs->egms/dot_general | solution.py:67
  152.2 0.1 multiply_reduce_fusion.5
  152.6 0.3 fusion.29
  152.9 1.7 %convolution_bitcast_fusion.2 = f32[64,2,4,128]{3,0,1,2:T(8,128)S(1)} fusion(f32[4,64,2,512]{3,1,2,0:T(8,128)S(1)} %fusion.29, bf16[4,512,128]{2,1,0:T(8,128)(2,1)} %get-tuple-element.391, f32[4,512]{1,0:T(4,128)S(1)} %get-tuple-element.390, bf16[4,32,512]{2,1,0:T(8,128)(2,1)S(1)} %get-tuple-element.389, bf16[64,2,4,32]{0,3,2,1:T(8,128)(2,1)S(1)} %bitcast.53), kind=kOutput, calls=%fused_computation.3.clone.1 | convolution fusion | flops 85721088 | bytes 2007040 | tf_op jit(solution)/shard_map/while/body/eval_jaxpr/egmh,mhs->egms/dot_general | solution.py:67
  154.7 0.1 multiply_reduce_fusion.5
  155.0 0.3 fusion.29
  155.3 1.7 %convolution_bitcast_fusion.2 = f32[64,2,4,128]{3,0,1,2:T(8,128)S(1)} fusion(f32[4,64,2,512]{3,1,2,0:T(8,128)S(1)} %fusion.29, bf16[4,512,128]{2,1,0:T(8,128)(2,1)} %get-tuple-element.391, f32[4,512]{1,0:T(4,128)S(1)} %get-tuple-element.390, bf16[4,32,512]{2,1,0:T(8,128)(2,1)S(1)} %get-tuple-element.389, bf16[64,2,4,32]{0,3,2,1:T(8,128)(2,1)S(1)} %bitcast.53), kind=kOutput, calls=%fused_computation.3.clone.1 | convolution fusion | flops 85721088 | bytes 2007040 | tf_op jit(solution)/shard_map/while/body/eval_jaxpr/egmh,mhs->egms/dot_general | solution.py:67
  157.1 0.1 multiply_reduce_fusion.5
  157.3 0.6 broadcast_multiply_fusion
  157.9 1.1 reduce_sum.79
  159.0 0.6 multiply_add_fusion
  (118 shorter events, 4.3 us)
Async XLA Ops:
  1.4 102.5 %copy-start.1 = (bf16[64,8,512]{2,1,0:T(8,128)(2,1)S(1)}, bf16[64,8,512]{2,1,0:T(8,128)(2,1)}, u32[]{:S(2)}) copy-start(bf16[64,8,512]{2,1,0:T(8,128)(2,1)} %param.14) | copy-start | bytes 1572868
  103.7 0.8 copy-start.2
  106.8 11.1 %copy-start = (bf16[4,128,512]{2,1,0:T(8,128)(2,1)S(1)}, bf16[4,128,512]{2,1,0:T(8,128)(2,1)}, u32[]{:S(2)}) copy-start(bf16[4,128,512]{2,1,0:T(8,128)(2,1)} %param.16) | copy-start | bytes 1572868
  106.8 11.1 %copy-start.5 = (bf16[4,32,512]{2,1,0:T(8,128)(2,1)S(1)}, bf16[4,32,512]{2,1,0:T(8,128)(2,1)}, u32[]{:S(2)}) copy-start(bf16[4,32,512]{2,1,0:T(8,128)(2,1)} %param.17) | copy-start | bytes 393220
  106.8 11.1 %copy-start.6 = (f32[4,512]{1,0:T(4,128)S(1)}, f32[4,512]{1,0:T(4,128)}, u32[]{:S(2)}) copy-start(f32[4,512]{1,0:T(4,128)} %param.18) | copy-start | bytes 24580
  107.7 50.2 %all-to-all-start = ((f32[64,1,1024]{2,1,0:T(1,128)}), f32[64,1,1024]{2,1,0:T(1,128)}, u32[]{:S(2)}, u32[]{:S(2)}) async-start(f32[64,1,1024]{2,1,0:T(1,128)} %copy.47), calls=%async_computation | async-start | bytes 524288 | tf_op jit(solution)/shard_map/all_to_all | solution.py:30
  117.9 41.2 %copy-start.3 = (f32[1,512]{1,0:T(1,128)S(1)}, f32[1,512]{1,0:T(1,128)}, u32[]{:S(2)}) copy-start(f32[1,512]{1,0:T(1,128)} %param.12) | copy-start | bytes 6148
  117.9 41.2 %copy-start.4 = (f32[1,512]{1,0:T(1,128)S(1)}, f32[1,512]{1,0:T(1,128)}, u32[]{:S(2)}) copy-start(f32[1,512]{1,0:T(1,128)} %param.11) | copy-start | bytes 6148
where the time goes:
time: 161 us; the launch traced here: 160 us
  blocking collectives  102 us (63%)
  matrix products  31.7 us (20%)
  other arithmetic  11.6 us (7%)
  starting transfers between devices  9.95 us (6%)
  local copies, waits for them, and re-layouts  2.27 us (1%)
    all_gather x1, blocking collectives, in_one_piece(): lax.all_gather(both, axis, axis=dim, tiled=True)  102 us
    dot_general x16, matrix products, advance(): jnp.einsum('egmh,mhs->egms', hidden, w_out, preferred_element_type=jnp.fl...  27 us
    all_to_all x1, starting transfers between devices, sent_and_summed(): lax.all_to_all(in_blocks(value, dim, devices), axis, 0, 0, tiled=True)  9.95 us
    dot_general x16, matrix products, advance(): jnp.einsum('egms,msh->egmh', grouped, w_state, preferred_element_type=jnp...  4.61 us
  transfers between devices with their start and end apart: 1, of which 0 were waited for; matrix products, arithmetic and copies ran while one was open for 24% of the time, Pallas kernels for 0%

commit v1 on v0

v1 whole, which is shorter than its diff:
```python
import functools

import jax
import jax.numpy as jnp
from jax import lax
from jax.experimental import pallas as pl
from jax.experimental.pallas import tpu as pltpu
from jax.sharding import PartitionSpec as P

BF = jnp.bfloat16
F32 = jnp.float32
ALPHA = 0.1
EPSILON = 1e-06
NX, NZ = 4, 16
ELITE, CAP, CD = 64, 4, 8
S, ADIM, HID, F, M, HOR = 128, 32, 512, 512, 4, 16
E = NX * NZ
ROW = 2 * F + S
NEAR = (1, 15, 2, 14, 3, 13, 4, 12, 5, 11, 6, 10, 7, 9, 8)


def kernel(
    mean_ref, var_ref, start_ref, noise_hbm, elite_ref, ws_hbm, wa_hbm, bias_ref, wo_hbm,
    ret_ref, nm_ref, nv_ref,
    rows, noise_v, noise_f, wide, eip, elites, arrived, sums, parts, w1, w2, act, states, energy,
    asum, perm,
    load_sem, zs, zr, xs, xr, ns, nr, ss, sr,
):
    me = lax.axis_index("cand")
    z, x = me // NX, me % NX

    def zpeer(d):
        return {"cand": ((z + d) % NZ) * NX + x}

    def xpeer(j):
        return {"cand": z * NX + (x + j) % NX}

    def remote(src, dst, send, recv, peer):
        return pltpu.make_async_remote_copy(
            src_ref=src, dst_ref=dst, send_sem=send, recv_sem=recv,
            device_id=peer, device_id_type=pl.DeviceIdType.MESH,
        )

    barrier = pltpu.get_barrier_semaphore()
    for d in NEAR[::-1]:
        pl.semaphore_signal(barrier, inc=1, device_id=zpeer(d), device_id_type=pl.DeviceIdType.MESH)
    for j in range(1, NX):
        pl.semaphore_signal(barrier, inc=1, device_id=xpeer(j), device_id_type=pl.DeviceIdType.MESH)

    loads = [pltpu.make_async_copy(noise_hbm, noise_v, load_sem.at[0])]
    for m in range(M):
        loads.append(pltpu.make_async_copy(wo_hbm.at[m], w2.at[m], load_sem.at[1 + m]))
        for r in range(4):
            n = 5 + 8 * m + 2 * r
            loads.append(
                pltpu.make_async_copy(ws_hbm.at[m], w1.at[m, r, pl.ds(0, S), :], load_sem.at[n])
            )
            loads.append(
                pltpu.make_async_copy(
                    wa_hbm.at[m], w1.at[m, r, pl.ds(S + ADIM * r, ADIM), :], load_sem.at[n + 1]
                )
            )
    for c in loads:
        c.start()

    rows[x, z, :, 0:F] = mean_ref[...]
    rows[x, z, :, F : 2 * F] = jnp.sqrt(var_ref[...])
    rows[x, z, :, 2 * F : ROW] = start_ref[...]

    for m in range(M):
        b = bias_ref[m : m + 1, :]
        hi = b.astype(BF).astype(F32)
        mid = (b - hi).astype(BF).astype(F32)
        low = b - hi - mid
        at = lax.broadcasted_iota(jnp.int32, (ADIM, HID), 0)
        tile = jnp.where(at == 0, hi, jnp.where(at == 1, mid, jnp.where(at == 2, low, 0.0)))
        tile = tile.astype(BF)
        for r in range(4):
            for k in range(4):
                if k != r:
                    w1[m, r, S + ADIM * k : S + ADIM * (k + 1), :] = (
                        tile if k == (r + 1) % 4 else jnp.zeros((ADIM, HID), BF)
                    )

    wide[...] = jnp.full((E, 128), -1, jnp.int32)
    wide[:, 0:ELITE] = elite_ref[...]
    for k in range(NX):
        eip[NZ * k : NZ * (k + 1), :] = wide[pl.ds(k, NZ, stride=NX), :]
    listed = eip[...]
    first = me * CD
    chosen = [
        jnp.sum(jnp.where(listed == first + c, 1.0, 0.0), axis=1, keepdims=True) for c in range(CD)
    ]
    ranks, total = [], jnp.zeros((E, 1), F32)
    for c in range(CD):
        ranks.append(total)
        total = total + chosen[c]

    loads[0].wait()
    for q in range(4):
        part = noise_v[:, :, 128 * q : 128 * (q + 1)]
        noise_f[q] = part.astype(F32).reshape(E * CD, 128)

    def drawn_by(k, c):
        at = pl.ds(k * CD + c, NZ, stride=NX * CD)
        return jnp.concatenate([noise_f[q, at, :] for q in range(4)], axis=1)

    for k in range(NX):
        for s in range(CAP):
            slot = jnp.zeros((NZ, F), F32)
            for c in range(s, CD):
                cut = slice(NZ * k, NZ * (k + 1))
                pick = jnp.where(ranks[c][cut] == float(s), chosen[c][cut], 0.0)
                slot = slot + pick * drawn_by(k, c)
            elites[k, s] = slot.astype(BF)

    pl.semaphore_wait(barrier, NZ - 1 + NX - 1)

    mine = rows.at[x, z]
    z_out = [remote(mine, mine, zs.at[d], zr.at[d], zpeer(d)) for d in NEAR[::-1]]
    for c in z_out:
        c.start()
    x_out = []
    for j in range(1, NX):
        x_out.append(remote(mine, mine, xs.at[0, j], xr.at[0, j], xpeer(j)))
        x_out[-1].start()
    n_out = []
    for j in range(1, NX):
        n_out.append(
            remote(elites.at[(x + j) % NX], arrived.at[j], ns.at[j], nr.at[j], xpeer(j))
        )
        n_out[-1].start()

    for d in NEAR:
        got = rows.at[x, (z - d + NZ) % NZ]
        remote(got, got, zs.at[d], zr.at[d], zpeer(d)).wait_recv()
        for j in range(1, NX):
            x_out.append(remote(got, got, xs.at[d, j], xr.at[d, j], xpeer(j)))
            x_out[-1].start()

    own = rows[x].reshape(NZ, ROW)
    line_mean, line_std = own[:, 0:F], own[:, F : 2 * F]
    line_listed = eip[pl.ds(pl.multiple_of(x * NZ, NZ), NZ), :] // CD
    first_sum = jnp.zeros((NZ, F), F32)
    second_sum = jnp.zeros((NZ, F), F32)
    for j in range(NX):
        block = z * NX + (x - j + NX) % NX
        count = jnp.sum(jnp.where(line_listed == block, 1.0, 0.0), axis=1, keepdims=True)
        if j > 0:
            n_out[j - 1].wait_recv()
        for s in range(CAP):
            drawn = (elites[x, s] if j == 0 else arrived[j, s]).astype(F32)
            a = jnp.clip(line_mean + line_std * drawn, -1.0, 1.0).astype(BF).astype(F32)
            a = jnp.where(count > float(s), a, 0.0)
            first_sum = first_sum + a
            second_sum = second_sum + a * a
    for k in range(4):
        cut = slice(128 * k, 128 * (k + 1))
        sums[pl.ds(k, NZ, stride=8), :] = first_sum[:, cut]
        sums[pl.ds(4 + k, NZ, stride=8), :] = second_sum[:, cut]

    def sum_copy(d):
        return remote(
            sums.at[pl.ds(pl.multiple_of(((z + d) % NZ) * 8, 8), 8), :],
            parts.at[pl.ds(8 * d, 8), :],
            ss.at[d], sr.at[d], zpeer(d),
        )

    s_out = [sum_copy(d) for d in NEAR[::-1]]
    for c in s_out:
        c.start()

    for d in (0,) + NEAR:
        for j in range(1, NX):
            got = rows.at[(x - j + NX) % NX, (z - d + NZ) % NZ]
            remote(got, got, xs.at[d, j], xr.at[d, j], xpeer(j)).wait_recv()

    gathered = [rows[k].reshape(NZ, ROW) for k in range(NX)]
    full_mean = jnp.concatenate([g[:, 0:F] for g in gathered], axis=0)
    full_std = jnp.concatenate([g[:, F : 2 * F] for g in gathered], axis=0)
    full_start = jnp.concatenate([g[:, 2 * F : ROW] for g in gathered], axis=0)
    for c in range(CD):
        m, h = c % M, c // M
        drawn = jnp.concatenate(
            [drawn_by(k, c) for k in range(NX)], axis=0
        )
        a = jnp.clip(full_mean + full_std * drawn, -1.0, 1.0).astype(BF).astype(F32)
        half = (0.5 * a).astype(BF)
        for q in range(4):
            act[m, q, E * h : E * (h + 1), :] = half[:, 128 * q : 128 * (q + 1)]
        asum[m, E * h : E * (h + 1), :] = jnp.sum(a * a, axis=1, keepdims=True)
        states[m, E * h : E * (h + 1), :] = full_start

    for c in loads[1:]:
        c.wait()
    lane = lax.broadcasted_iota(jnp.int32, (2 * E, 128), 1)

    def squares(s):
        return jnp.sum(s * s, axis=1, keepdims=True)

    def step(q, r):
        left = []
        for m in range(M):
            s = states[m]
            e = squares(s)
            energy[m] = energy[m] + e
            n = (s * (0.5 * lax.rsqrt(e * (1.0 / S) + EPSILON))).astype(BF)
            at = ADIM * ((r + 1) % 4)
            ones = jnp.where((lane >= at) & (lane < at + 3), 0.5, 0.0).astype(BF)
            now = (lane >= ADIM * r) & (lane < ADIM * (r + 1))
            left.append((s, jnp.concatenate([n, jnp.where(now, act[m, q], ones)], axis=1)))
        halves = [
            jnp.dot(left[m][1], w1[m, r], preferred_element_type=F32) for m in range(M)
        ]
        for m in range(M):
            h = halves[m]
            hidden = (h + h * jnp.tanh(h)).astype(BF)
            states[m] = left[m][0] + jnp.dot(hidden, w2[m], preferred_element_type=F32)

    initial = squares(full_start)
    for m in range(M):
        energy[m] = -jnp.concatenate([initial, initial], axis=0)

    def quarter(q, carry):
        for r in range(4):
            step(q, r)
        return carry

    lax.fori_loop(0, 4, quarter, 0)

    out_lane = lax.broadcasted_iota(jnp.int32, (E, 128), 1)
    table = jnp.zeros((E, 128), F32)
    for c in range(CD):
        m, h = c % M, c // M
        cut = slice(E * h, E * (h + 1))
        e = energy[m, cut, :] + squares(states[m, cut, :])
        value = e * (-1.0 / (S * HOR)) - asum[m, cut, :] * (0.1 / (ADIM * HOR))
        table = jnp.where(out_lane == c, value, table)
    for k in range(NX):
        perm[pl.ds(k, NZ, stride=NX), :] = table[NZ * k : NZ * (k + 1), :]
    ret_ref[...] = perm[:, 0:CD]

    total = sums[pl.ds(pl.multiple_of(z * 8, 8), 8), :]
    for d in NEAR:
        sum_copy(d).wait_recv()
        total = total + parts[8 * d : 8 * (d + 1), :]
    for k in range(4):
        cut = slice(128 * k, 128 * (k + 1))
        elite_mean = total[k : k + 1, :] * (1.0 / ELITE)
        elite_var = total[4 + k : 5 + k, :] * (1.0 / ELITE) - elite_mean * elite_mean
        nm_ref[:, cut] = ALPHA * mean_ref[:, cut] + (1.0 - ALPHA) * elite_mean
        nv_ref[:, cut] = ALPHA * var_ref[:, cut] + (1.0 - ALPHA) * elite_var

    for c in z_out + x_out + n_out + s_out:
        c.wait_send()


def per_device(mean, var, start, noise, elite, w_state, w_act, bias, w_out):
    vmem = pl.BlockSpec(memory_space=pltpu.VMEM)
    hbm = pl.BlockSpec(memory_space=pl.ANY)
    dma = pltpu.SemaphoreType.DMA
    return pl.pallas_call(
        kernel,
        out_shape=(
            jax.ShapeDtypeStruct((E, CD), F32),
            jax.ShapeDtypeStruct((1, F), F32),
            jax.ShapeDtypeStruct((1, F), F32),
        ),
        in_specs=[vmem, vmem, vmem, hbm, vmem, hbm, hbm, vmem, hbm],
        out_specs=(vmem, vmem, vmem),
        scratch_shapes=[
            pltpu.VMEM((NX, NZ, 1, ROW), F32),
            pltpu.VMEM((E, CD, F), BF),
            pltpu.VMEM((4, E * CD, 128), F32),
            pltpu.VMEM((E, 128), jnp.int32),
            pltpu.VMEM((E, 128), jnp.int32),
            pltpu.VMEM((NX, CAP, NZ, F), BF),
            pltpu.VMEM((NX, CAP, NZ, F), BF),
            pltpu.VMEM((NZ * 8, 128), F32),
            pltpu.VMEM((NZ * 8, 128), F32),
            pltpu.VMEM((M, 4, 2 * S, HID), BF),
            pltpu.VMEM((M, HID, S), BF),
            pltpu.VMEM((M, 4, 2 * E, 128), BF),
            pltpu.VMEM((M, 2 * E, S), F32),
            pltpu.VMEM((M, 2 * E, 1), F32),
            pltpu.VMEM((M, 2 * E, 1), F32),
            pltpu.VMEM((E, 128), F32),
            dma((37,)), dma((NZ,)), dma((NZ,)), dma((NZ, NX)), dma((NZ, NX)),
            dma((NX,)), dma((NX,)), dma((NZ,)), dma((NZ,)),
        ],
        compiler_params=pltpu.CompilerParams(
            collective_id=0, has_side_effects=True, vmem_limit_bytes=48 * 2**20
        ),
    )(mean, var, start, noise, elite, w_state, w_act, bias, w_out)


def solution(mesh):
    both = P(("env", "cand"), None)
    in_specs = (both, both, both, P("env", "cand", None), P("env", None), P(), P(), P(), P())
    return jax.shard_map(
        per_device, mesh=mesh, in_specs=in_specs, out_specs=(P("env", "cand"), both, both),
        check_vma=False,
    )
```

time: 161 us -> 48.6 us (0.30)
  blocking collectives: 102 us -> 0 us
  Pallas kernels: 0 us -> 38.1 us
  matrix products: 31.7 us -> 0 us
  other arithmetic: 11.6 us -> 0 us
  starting transfers between devices: 9.95 us -> 0 us
  local copies, waits for them, and re-layouts: 2.27 us -> 9.31 us
    all_gather x1 -> x0, blocking collectives: 102 us -> none  [in_one_piece(): lax.all_gather(both, axis, axis=dim, tiled=True)]
    pallas_call x0 -> x1, Pallas kernels: none -> 38.1 us  [per_device(): pl.pallas_call(kernel, out_shape=(jax.ShapeDtypeStruct((E, CD), F32), jax...]
    dot_general x32 -> x0, matrix products: 31.7 us -> none  [the longest x16 27 us: advance(): jnp.einsum('egmh,mhs->egms', hidden, w_out, preferred_element_type=jnp.fl...]
    all_to_all x1 -> x0, starting transfers between devices: 9.95 us -> none  [sent_and_summed(): lax.all_to_all(in_blocks(value, dim, devices), axis, 0, 0, tiled=True)]
    unnamed x16 -> x20, local copies, waits for them, and re-layouts: 0.71 us -> 8.65 us
    reduce_sum x35 -> x0, other arithmetic: 4.92 us -> none  [the longest x16 2.22 us: advance(): jnp.mean(states * states, axis=-1)]
    convert_element_type x17 -> x0, other arithmetic: 2.15 us -> none  [the longest x16 2.15 us: advance(): normed = (states * lax.rsqrt(energy)).astype(jnp.bfloat16)]
    add x34 -> x0, other arithmetic: 1.81 us -> none  [the longest x16 1.09 us: advance(): states = states + change.reshape(env_count, cand_count, features)]
  transfers between devices with their start and end apart: 1 -> 0, of which waited for: 0 -> 0; matrix products, arithmetic and copies ran while one was open for 24% -> 0% of each run, Pallas kernels for 0% -> 0%
where the time goes in v1:
time: 48.6 us; the launch traced here: 48.1 us
  Pallas kernels  38.1 us (78%)
  local copies, waits for them, and re-layouts  9.31 us (19%)
  between operations  0.66 us (1%)
    pallas_call x1, Pallas kernels, per_device(): pl.pallas_call(kernel, out_shape=(jax.ShapeDtypeStruct((E, CD), F32), jax...  38.1 us
    unnamed x20, local copies, waits for them, and re-layouts  8.65 us

profile of v1, /device:TPU:24, one launch (start us, length us, event | category | flops | bytes accessed | tf_op | source)
XLA Modules:
  0.0 48.1 jit_solution(10194915523273706291)
XLA Ops:
  0.6 0.0 copy-start
  0.6 1.0 %copy-done = bf16[64,8,512]{2,1,0:T(8,128)(2,1)S(1)} copy-done((bf16[64,8,512]{2,1,0:T(8,128)(2,1)S(1)}, bf16[64,8,512]{2,1,0:T(8,128)(2,1)}, u32[]{:S(2)}) %copy-start) | copy-done | bytes 524312
  1.7 0.0 copy-start.1
  1.7 1.0 %copy-done.1 = bf16[4,128,512]{2,1,0:T(8,128)(2,1)S(1)} copy-done((bf16[4,128,512]{2,1,0:T(8,128)(2,1)S(1)}, bf16[4,128,512]{2,1,0:T(8,128)(2,1)}, u32[]{:S(2)}) %copy-start.1) | copy-done | bytes 524312
  2.7 0.0 copy-start.2
  2.7 1.0 %copy-done.2 = bf16[4,512,128]{2,1,0:T(8,128)(2,1)S(1)} copy-done((bf16[4,512,128]{2,1,0:T(8,128)(2,1)S(1)}, bf16[4,512,128]{2,1,0:T(8,128)(2,1)}, u32[]{:S(2)}) %copy-start.2) | copy-done | bytes 524312
  3.8 0.0 copy-start.3
  3.8 0.9 %copy-done.3 = bf16[4,32,512]{2,1,0:T(8,128)(2,1)S(1)} copy-done((bf16[4,32,512]{2,1,0:T(8,128)(2,1)S(1)}, bf16[4,32,512]{2,1,0:T(8,128)(2,1)}, u32[]{:S(2)}) %copy-start.3) | copy-done | bytes 131096
  4.7 0.0 copy-start.4
  4.7 0.8 %copy-done.4 = s32[64,64]{1,0:T(8,128)S(1)} copy-done((s32[64,64]{1,0:T(8,128)S(1)}, s32[64,64]{1,0:T(8,128)}, u32[]{:S(2)}) %copy-start.4) | copy-done | bytes 16408
  5.4 0.0 copy-start.5
  5.4 0.7 %copy-done.5 = f32[4,512]{1,0:T(4,128)S(1)} copy-done((f32[4,512]{1,0:T(4,128)S(1)}, f32[4,512]{1,0:T(4,128)}, u32[]{:S(2)}) %copy-start.5) | copy-done | bytes 8216
  6.1 0.0 copy-start.6
  6.1 0.7 %copy-done.6 = f32[1,512]{1,0:T(1,128)S(1)} copy-done((f32[1,512]{1,0:T(1,128)S(1)}, f32[1,512]{1,0:T(1,128)}, u32[]{:S(2)}) %copy-start.6) | copy-done | bytes 2072
  6.8 0.0 copy-start.7
  6.8 0.7 %copy-done.7 = f32[1,512]{1,0:T(1,128)S(1)} copy-done((f32[1,512]{1,0:T(1,128)S(1)}, f32[1,512]{1,0:T(1,128)}, u32[]{:S(2)}) %copy-start.7) | copy-done | bytes 2072
  7.5 0.0 copy-start.8
  7.5 0.7 %copy-done.8 = f32[1,128]{1,0:T(1,128)S(1)} copy-done((f32[1,128]{1,0:T(1,128)S(1)}, f32[1,128]{1,0:T(1,128)}, u32[]{:S(2)}) %copy-start.8) | copy-done | bytes 536
  8.1 38.1 %shard_map.112 = (f32[64,8]{1,0:T(8,128)S(1)}, f32[1,512]{1,0:T(1,128)S(1)}, f32[1,512]{1,0:T(1,128)S(1)}) custom-call(f32[1,512]{1,0:T(1,128)S(1)} %copy-done.6, f32[1,512]{1,0:T(1,128)S(1)} %copy-done.7, f32[1,128]{1,0:T(1,128)S(1)} %copy-done.8, bf16[64,8,512]{2,1,0:T(8,128)(2,1)S(1)} %copy-done, s32[64,64]{1,0:T(8,128)S(1)} %copy-done.4, ...), custom_call_target="tpu_custom_call" | custom-call | tf_op jit(solution)/shard_map/pallas_call | solution.py:262
  46.3 0.7 %copy.12 = f32[64,8]{0,1:T(8,128)} copy(f32[64,8]{1,0:T(8,128)S(1)} %get-tuple-element.3) | data formatting | bytes 4096 | tf_op jit(solution)/shard_map/pallas_call | solution.py:262
  47.0 0.6 %copy.15 = f32[1,512]{1,0:T(1,128)} copy(f32[1,512]{1,0:T(1,128)S(1)} %get-tuple-element.10) | data formatting | bytes 4096
  47.5 0.6 %copy.16 = f32[1,512]{1,0:T(1,128)} copy(f32[1,512]{1,0:T(1,128)S(1)} %get-tuple-element.11) | data formatting | bytes 4096
Async XLA Ops:
  0.6 1.0 %copy-start = (bf16[64,8,512]{2,1,0:T(8,128)(2,1)S(1)}, bf16[64,8,512]{2,1,0:T(8,128)(2,1)}, u32[]{:S(2)}) copy-start(bf16[64,8,512]{2,1,0:T(8,128)(2,1)} %noise_hbm.1) | copy-start | bytes 1572868
  1.7 1.0 %copy-start.1 = (bf16[4,128,512]{2,1,0:T(8,128)(2,1)S(1)}, bf16[4,128,512]{2,1,0:T(8,128)(2,1)}, u32[]{:S(2)}) copy-start(bf16[4,128,512]{2,1,0:T(8,128)(2,1)} %ws_hbm.1) | copy-start | bytes 1572868
  2.7 1.0 %copy-start.2 = (bf16[4,512,128]{2,1,0:T(8,128)(2,1)S(1)}, bf16[4,512,128]{2,1,0:T(8,128)(2,1)}, u32[]{:S(2)}) copy-start(bf16[4,512,128]{2,1,0:T(8,128)(2,1)} %wo_hbm.1) | copy-start | bytes 1572868
  3.8 0.9 %copy-start.3 = (bf16[4,32,512]{2,1,0:T(8,128)(2,1)S(1)}, bf16[4,32,512]{2,1,0:T(8,128)(2,1)}, u32[]{:S(2)}) copy-start(bf16[4,32,512]{2,1,0:T(8,128)(2,1)} %wa_hbm.1) | copy-start | bytes 393220
  4.7 0.8 %copy-start.4 = (s32[64,64]{1,0:T(8,128)S(1)}, s32[64,64]{1,0:T(8,128)}, u32[]{:S(2)}) copy-start(s32[64,64]{1,0:T(8,128)} %elite_ref.1) | copy-start | bytes 49156
  5.4 0.7 %copy-start.5 = (f32[4,512]{1,0:T(4,128)S(1)}, f32[4,512]{1,0:T(4,128)}, u32[]{:S(2)}) copy-start(f32[4,512]{1,0:T(4,128)} %bias_ref.1) | copy-start | bytes 24580
  6.1 0.7 %copy-start.6 = (f32[1,512]{1,0:T(1,128)S(1)}, f32[1,512]{1,0:T(1,128)}, u32[]{:S(2)}) copy-start(f32[1,512]{1,0:T(1,128)} %mean_ref.1) | copy-start | bytes 6148
  6.8 0.7 %copy-start.7 = (f32[1,512]{1,0:T(1,128)S(1)}, f32[1,512]{1,0:T(1,128)}, u32[]{:S(2)}) copy-start(f32[1,512]{1,0:T(1,128)} %var_ref.1) | copy-start | bytes 6148
  7.5 0.7 %copy-start.8 = (f32[1,128]{1,0:T(1,128)S(1)}, f32[1,128]{1,0:T(1,128)}, u32[]{:S(2)}) copy-start(f32[1,128]{1,0:T(1,128)} %start_ref.1) | copy-start | bytes 1540

commit v2 on v1

--- a/solution.py
+++ b/solution.py
@@ -16,13 +16,16 @@
 S, ADIM, HID, F, M, HOR = 128, 32, 512, 512, 4, 16
 E = NX * NZ
 ROW = 2 * F + S
-NEAR = (1, 15, 2, 14, 3, 13, 4, 12, 5, 11, 6, 10, 7, 9, 8)
+REACH = 4
+DIRECT = (1, 15, 2, 14, 3, 13, 4, 12)
+RELAYED = (5, 11, 6, 10, 7, 9, 8)
+NEAR = DIRECT + RELAYED
 
 
 def kernel(
-    mean_ref, var_ref, start_ref, noise_hbm, elite_ref, ws_hbm, wa_hbm, bias_ref, wo_hbm,
+    mean_hbm, var_hbm, start_hbm, noise_hbm, elite_hbm, ws_hbm, wa_hbm, bias_hbm, wo_hbm,
     ret_ref, nm_ref, nv_ref,
-    rows, noise_v, noise_f, wide, eip, elites, arrived, sums, parts, w1, w2, act, states, energy,
+    mean_ref, var_ref, start_ref, elite_ref, bias_ref, rows, noise_v, noise_f, wide, eip, elites, arrived, sums, parts, w1, w2, act, states, energy,
     asum, perm,
     load_sem, zs, zr, xs, xr, ns, nr, ss, sr,
 ):
@@ -42,11 +45,20 @@
         )
 
     barrier = pltpu.get_barrier_semaphore()
-    for d in NEAR[::-1]:
+    for d in DIRECT[::-1]:
         pl.semaphore_signal(barrier, inc=1, device_id=zpeer(d), device_id_type=pl.DeviceIdType.MESH)
     for j in range(1, NX):
         pl.semaphore_signal(barrier, inc=1, device_id=xpeer(j), device_id_type=pl.DeviceIdType.MESH)
 
+    small = [
+        pltpu.make_async_copy(src, dst, load_sem.at[37 + i])
+        for i, (src, dst) in enumerate(
+            ((mean_hbm, mean_ref), (var_hbm, var_ref), (start_hbm, start_ref),
+             (bias_hbm, bias_ref), (elite_hbm, elite_ref))
+        )
+    ]
+    for c in small:
+        c.start()
     loads = [pltpu.make_async_copy(noise_hbm, noise_v, load_sem.at[0])]
     for m in range(M):
         loads.append(pltpu.make_async_copy(wo_hbm.at[m], w2.at[m], load_sem.at[1 + m]))
@@ -63,9 +75,60 @@
     for c in loads:
         c.start()
 
+    for c in small:
+        c.wait()
     rows[x, z, :, 0:F] = mean_ref[...]
     rows[x, z, :, F : 2 * F] = jnp.sqrt(var_ref[...])
     rows[x, z, :, 2 * F : ROW] = start_ref[...]
+
+    pl.semaphore_wait(barrier, len(DIRECT) + NX - 1)
+
+    mine = rows.at[x, z]
+    z_out = [remote(mine, mine, zs.at[d], zr.at[d], zpeer(d)) for d in DIRECT[::-1]]
+    for c in z_out:
+        c.start()
+    x_out = []
+    for j in range(1, NX):
+        x_out.append(remote(mine, mine, xs.at[0, j], xr.at[0, j], xpeer(j)))
+        x_out[-1].start()
+    wide[...] = jnp.full((E, 128), -1, jnp.int32)
+    wide[:, 0:ELITE] = elite_ref[...]
+    for k in range(NX):
+        eip[NZ * k : NZ * (k + 1), :] = wide[pl.ds(k, NZ, stride=NX), :]
+    listed = eip[...]
+    first = me * CD
+    chosen = [
+        jnp.sum(jnp.where(listed == first + c, 1.0, 0.0), axis=1, keepdims=True) for c in range(CD)
+    ]
+    ranks, total = [], jnp.zeros((E, 1), F32)
+    for c in range(CD):
+        ranks.append(total)
+        total = total + chosen[c]
+
+    loads[0].wait()
+    for q in range(4):
+        part = noise_v[:, :, 128 * q : 128 * (q + 1)]
+        noise_f[q] = part.astype(F32).reshape(E * CD, 128)
+
+    def drawn_by(k, c):
+        at = pl.ds(k * CD + c, NZ, stride=NX * CD)
+        return jnp.concatenate([noise_f[q, at, :] for q in range(4)], axis=1)
+
+    for k in range(NX):
+        for s in range(CAP):
+            slot = jnp.zeros((NZ, F), F32)
+            for c in range(s, CD):
+                cut = slice(NZ * k, NZ * (k + 1))
+                pick = jnp.where(ranks[c][cut] == float(s), chosen[c][cut], 0.0)
+                slot = slot + pick * drawn_by(k, c)
+            elites[k, s] = slot.astype(BF)
+
+    n_out = []
+    for j in range(1, NX):
+        n_out.append(
+            remote(elites.at[(x + j) % NX], arrived.at[j], ns.at[j], nr.at[j], xpeer(j))
+        )
+        n_out[-1].start()
 
     for m in range(M):
         b = bias_ref[m : m + 1, :]
@@ -82,58 +145,14 @@
                         tile if k == (r + 1) % 4 else jnp.zeros((ADIM, HID), BF)
                     )
 
-    wide[...] = jnp.full((E, 128), -1, jnp.int32)
-    wide[:, 0:ELITE] = elite_ref[...]
-    for k in range(NX):
-        eip[NZ * k : NZ * (k + 1), :] = wide[pl.ds(k, NZ, stride=NX), :]
-    listed = eip[...]
-    first = me * CD
-    chosen = [
-        jnp.sum(jnp.where(listed == first + c, 1.0, 0.0), axis=1, keepdims=True) for c in range(CD)
-    ]
-    ranks, total = [], jnp.zeros((E, 1), F32)
-    for c in range(CD):
-        ranks.append(total)
-        total = total + chosen[c]
-
-    loads[0].wait()
-    for q in range(4):
-        part = noise_v[:, :, 128 * q : 128 * (q + 1)]
-        noise_f[q] = part.astype(F32).reshape(E * CD, 128)
-
-    def drawn_by(k, c):
-        at = pl.ds(k * CD + c, NZ, stride=NX * CD)
-        return jnp.concatenate([noise_f[q, at, :] for q in range(4)], axis=1)
-
-    for k in range(NX):
-        for s in range(CAP):
-            slot = jnp.zeros((NZ, F), F32)
-            for c in range(s, CD):
-                cut = slice(NZ * k, NZ * (k + 1))
-                pick = jnp.where(ranks[c][cut] == float(s), chosen[c][cut], 0.0)
-                slot = slot + pick * drawn_by(k, c)
-            elites[k, s] = slot.astype(BF)
-
-    pl.semaphore_wait(barrier, NZ - 1 + NX - 1)
-
-    mine = rows.at[x, z]
-    z_out = [remote(mine, mine, zs.at[d], zr.at[d], zpeer(d)) for d in NEAR[::-1]]
-    for c in z_out:
-        c.start()
-    x_out = []
-    for j in range(1, NX):
-        x_out.append(remote(mine, mine, xs.at[0, j], xr.at[0, j], xpeer(j)))
-        x_out[-1].start()
-    n_out = []
-    for j in range(1, NX):
-        n_out.append(
-            remote(elites.at[(x + j) % NX], arrived.at[j], ns.at[j], nr.at[j], xpeer(j))
-        )
-        n_out[-1].start()
-
     for d in NEAR:
         got = rows.at[x, (z - d + NZ) % NZ]
         remote(got, got, zs.at[d], zr.at[d], zpeer(d)).wait_recv()
+        if d <= REACH or NZ - REACH < d:
+            onward = REACH if d <= REACH else NZ - REACH
+            far = (d + onward) % NZ
+            z_out.append(remote(got, got, zs.at[far], zr.at[far], zpeer(onward)))
+            z_out[-1].start()
         for j in range(1, NX):
             x_out.append(remote(got, got, xs.at[d, j], xr.at[d, j], xpeer(j)))
             x_out[-1].start()
@@ -238,7 +257,7 @@
         table = jnp.where(out_lane == c, value, table)
     for k in range(NX):
         perm[pl.ds(k, NZ, stride=NX), :] = table[NZ * k : NZ * (k + 1), :]
-    ret_ref[...] = perm[:, 0:CD]
+    ret_ref[...] = perm[...].T[0:CD, 0:E]
 
     total = sums[pl.ds(pl.multiple_of(z * 8, 8), 8), :]
     for d in NEAR:
@@ -255,20 +274,39 @@
         c.wait_send()
 
 
+def put_out(a, b, c, a_out, b_out, c_out, a_v, b_v, c_v, sem):
+    trips = ((a, a_v, a_out), (b, b_v, b_out), (c, c_v, c_out))
+    taken = [pltpu.make_async_copy(src, mid, sem.at[i]) for i, (src, mid, _) in enumerate(trips)]
+    given = [pltpu.make_async_copy(mid, dst, sem.at[i]) for i, (_, mid, dst) in enumerate(trips)]
+    for copy in taken:
+        copy.start()
+    for i in range(3):
+        taken[i].wait()
+        given[i].start()
+    for copy in given:
+        copy.wait()
+
+
 def per_device(mean, var, start, noise, elite, w_state, w_act, bias, w_out):
     vmem = pl.BlockSpec(memory_space=pltpu.VMEM)
     hbm = pl.BlockSpec(memory_space=pl.ANY)
     dma = pltpu.SemaphoreType.DMA
-    return pl.pallas_call(
-        kernel,
-        out_shape=(
-            jax.ShapeDtypeStruct((E, CD), F32),
+    shapes = (
+            jax.ShapeDtypeStruct((CD, E), F32),
             jax.ShapeDtypeStruct((1, F), F32),
             jax.ShapeDtypeStruct((1, F), F32),
-        ),
-        in_specs=[vmem, vmem, vmem, hbm, vmem, hbm, hbm, vmem, hbm],
+        )
+    results = pl.pallas_call(
+        kernel,
+        out_shape=shapes,
+        in_specs=[hbm] * 9,
         out_specs=(vmem, vmem, vmem),
         scratch_shapes=[
+            pltpu.VMEM((1, F), F32),
+            pltpu.VMEM((1, F), F32),
+            pltpu.VMEM((1, S), F32),
+            pltpu.VMEM((E, ELITE), jnp.int32),
+            pltpu.VMEM((M, HID), F32),
             pltpu.VMEM((NX, NZ, 1, ROW), F32),
             pltpu.VMEM((E, CD, F), BF),
             pltpu.VMEM((4, E * CD, 128), F32),
@@ -284,14 +322,23 @@
             pltpu.VMEM((M, 2 * E, S), F32),
             pltpu.VMEM((M, 2 * E, 1), F32),
             pltpu.VMEM((M, 2 * E, 1), F32),
-            pltpu.VMEM((E, 128), F32),
-            dma((37,)), dma((NZ,)), dma((NZ,)), dma((NZ, NX)), dma((NZ, NX)),
+            pltpu.VMEM((128, 128), F32),
+            dma((42,)), dma((NZ,)), dma((NZ,)), dma((NZ, NX)), dma((NZ, NX)),
             dma((NX,)), dma((NX,)), dma((NZ,)), dma((NZ,)),
         ],
         compiler_params=pltpu.CompilerParams(
-            collective_id=0, has_side_effects=True, vmem_limit_bytes=48 * 2**20
+            collective_id=0, has_side_effects=True, vmem_limit_bytes=60 * 1024 * 2**10
         ),
     )(mean, var, start, noise, elite, w_state, w_act, bias, w_out)
+    returns, new_mean, new_var = pl.pallas_call(
+        put_out,
+        out_shape=shapes,
+        in_specs=[hbm] * 3,
+        out_specs=(hbm, hbm, hbm),
+        scratch_shapes=[pltpu.VMEM(s.shape, s.dtype) for s in shapes] + [dma((3,))],
+        compiler_params=pltpu.CompilerParams(vmem_limit_bytes=60 * 1024 * 2**10),
+    )(*results)
+    return returns.T, new_mean, new_var
 
 
 def solution(mesh):

time: 48.6 us -> 38.6 us (0.79)
  local copies, waits for them, and re-layouts: 9.31 us -> 0 us
    unnamed x20 -> x0, local copies, waits for them, and re-layouts: 8.65 us -> none
    pallas_call x1 -> x0, local copies, waits for them, and re-layouts: 0.66 us -> none  [per_device(): pl.pallas_call(kernel, out_shape=(jax.ShapeDtypeStruct((E, CD), F32), jax...]
    pallas_call x1 -> x2, Pallas kernels: 38.1 us -> 37.8 us  [the longest x1 36.5 us: per_device(): pl.pallas_call(kernel, out_shape=shapes, in_specs=[hbm] * 9, out_specs=(v...]
where the time goes in v2:
time: 38.6 us; the launch traced here: 38.4 us
  Pallas kernels  37.8 us (98%)
  between operations  0.64 us (2%)
    pallas_call x1, Pallas kernels, per_device(): pl.pallas_call(kernel, out_shape=shapes, in_specs=[hbm] * 9, out_specs=(v...  36.5 us
    pallas_call x1, Pallas kernels, per_device(): pl.pallas_call(put_out, out_shape=shapes, in_specs=[hbm] * 3, out_specs=(...  1.29 us

profile of v2, /device:TPU:24, one launch (start us, length us, event | category | flops | bytes accessed | tf_op | source)
XLA Modules:
  0.0 38.4 jit_solution(17432788244824720436)
XLA Ops:
  0.6 36.5 %shard_map.112 = (f32[8,64]{1,0:T(8,128)}, f32[1,512]{1,0:T(1,128)}, f32[1,512]{1,0:T(1,128)}) custom-call(f32[1,512]{1,0:T(1,128)} %mean_hbm.1, f32[1,512]{1,0:T(1,128)} %var_hbm.1, f32[1,128]{1,0:T(1,128)} %start_hbm.1, bf16[64,8,512]{2,1,0:T(8,128)(2,1)} %noise_hbm.1, s32[64,64]{1,0:T(8,128)} %elite_hbm.1, bf16[4,128,512]{2,1,0:T(8,128)(2,1)} %ws_hbm.1, ...), custom_call_target="tpu_custom_call" | custom-call | tf_op jit(solution)/shard_map/pallas_call | solution.py:299
  37.1 1.3 %shard_map.113 = (f32[8,64]{1,0:T(8,128)}, f32[1,512]{1,0:T(1,128)}, f32[1,512]{1,0:T(1,128)}) custom-call(f32[8,64]{1,0:T(8,128)} %get-tuple-element.9.a, f32[1,512]{1,0:T(1,128)} %get-tuple-element.10.b, f32[1,512]{1,0:T(1,128)} %get-tuple-element.11.c), custom_call_target="tpu_custom_call" | custom-call | tf_op jit(solution)/shard_map/pallas_call | solution.py:333

commit v3 on v2

v3 whole, which is shorter than its diff:
```python
import functools

import jax
import jax.numpy as jnp
from jax import lax
from jax.experimental import pallas as pl
from jax.experimental.pallas import tpu as pltpu
from jax.sharding import PartitionSpec as P

BF = jnp.bfloat16
F32 = jnp.float32
ALPHA = 0.1
EPSILON = 1e-06
NX, NZ = 4, 16
ELITE, CAP, CD = 64, 4, 8
S, ADIM, HID, F, M, HOR = 128, 32, 512, 512, 4, 16
E = NX * NZ
ROW = 2 * F + S
REACH = 4
DIRECT = (1, 15, 2, 14, 3, 13, 4, 12)
RELAYED = (5, 11, 6, 10, 7, 9, 8)
NEAR = DIRECT + RELAYED


def kernel(
    mean_hbm, var_hbm, start_hbm, noise_hbm, elite_hbm, ws_hbm, wa_hbm, bias_hbm, wo_hbm,
    ret_ref, nm_ref, nv_ref,
    mean_ref, var_ref, start_ref, elite_ref, bias_ref, rows, noise_v, noise_f, wide, eip, elites, arrived, sums, parts, w1, w2, act, states, energy,
    asum, perm,
    load_sem, zs, zr, xs, xr, ns, nr, ss, sr,
):
    me = lax.axis_index("cand")
    z, x = lax.div(me, NX), lax.rem(me, NX)

    def zpeer(d):
        return {"cand": lax.rem(me + NX * d, E)}

    def xpeer(j):
        return {"cand": z * NX + lax.rem(x + j, NX)}

    def zback(d):
        return lax.rem(z + NZ - d, NZ)

    def xback(j):
        return lax.rem(x + NX - j, NX)

    def remote(src, dst, send, recv, peer):
        return pltpu.make_async_remote_copy(
            src_ref=src, dst_ref=dst, send_sem=send, recv_sem=recv,
            device_id=peer, device_id_type=pl.DeviceIdType.MESH,
        )

    small = [
        pltpu.make_async_copy(src, dst, load_sem.at[i])
        for i, (src, dst) in enumerate(
            ((mean_hbm, mean_ref), (var_hbm, var_ref), (start_hbm, start_ref),
             (bias_hbm, bias_ref), (elite_hbm, elite_ref), (noise_hbm, noise_v))
        )
    ]
    for c in small[:3]:
        c.start()
    barrier = pltpu.get_barrier_semaphore()
    for d in DIRECT[::-1]:
        pl.semaphore_signal(barrier, inc=1, device_id=zpeer(d), device_id_type=pl.DeviceIdType.MESH)
    for j in range(1, NX):
        pl.semaphore_signal(barrier, inc=1, device_id=xpeer(j), device_id_type=pl.DeviceIdType.MESH)
    for c in small[3:]:
        c.start()

    for c in small[:3]:
        c.wait()
    rows[x, z, :, 0:F] = mean_ref[...]
    rows[x, z, :, F : 2 * F] = jnp.sqrt(var_ref[...])
    rows[x, z, :, 2 * F : ROW] = start_ref[...]

    pl.semaphore_wait(barrier, len(DIRECT) + NX - 1)

    mine = rows.at[x, z]
    for d in DIRECT[::-1]:
        remote(mine, mine, zs, zr.at[d], zpeer(d)).start()
    for j in range(1, NX):
        remote(mine, mine, xs, xr.at[j], xpeer(j)).start()

    for m in range(M):
        pltpu.make_async_copy(wo_hbm.at[m], w2.at[m], load_sem.at[6]).start()
        for r in range(4):
            pltpu.make_async_copy(ws_hbm.at[m], w1.at[m, r, 0:S, :], load_sem.at[7]).start()
            rest = w1.at[m, r, S + ADIM * r : S + ADIM * (r + 1), :]
            pltpu.make_async_copy(wa_hbm.at[m], rest, load_sem.at[7]).start()

    small[4].wait()
    wide[...] = jnp.full((E, 128), -1, jnp.int32)
    wide[:, 0:ELITE] = elite_ref[...]
    for k in range(NX):
        eip[NZ * k : NZ * (k + 1), :] = wide[pl.ds(k, NZ, stride=NX), :]

    small[5].wait()
    for q in range(4):
        part = noise_v[:, :, 128 * q : 128 * (q + 1)]
        noise_f[q] = part.astype(F32).reshape(E * CD, 128)

    def drawn_by(k, c):
        at = pl.ds(k * CD + c, NZ, stride=NX * CD)
        return jnp.concatenate([noise_f[q, at, :] for q in range(4)], axis=1)

    for k in range(NX):
        listed = eip[NZ * k : NZ * (k + 1), :]
        before = jnp.zeros((NZ, 1), F32)
        slots = [jnp.zeros((NZ, F), F32) for _ in range(CAP)]
        for c in range(CD):
            hit = jnp.where(listed == me * CD + c, 1.0, 0.0)
            chosen = jnp.sum(hit, axis=1, keepdims=True)
            drawn = drawn_by(k, c)
            place = jnp.where(chosen > 0.5, before, -1.0)
            for s in range(min(c + 1, CAP)):
                slots[s] = jnp.where(place == float(s), drawn, slots[s])
            before = before + chosen
        for s in range(CAP):
            elites[k, s] = slots[s].astype(BF)

    for j in range(1, NX):
        remote(elites.at[lax.rem(x + j, NX)], arrived.at[j], ns, nr.at[j], xpeer(j)).start()

    small[3].wait()
    for m in range(M):
        b = bias_ref[m : m + 1, :]
        hi = b.astype(BF).astype(F32)
        mid = (b - hi).astype(BF).astype(F32)
        low = b - hi - mid
        at = lax.broadcasted_iota(jnp.int32, (ADIM, HID), 0)
        tile = jnp.where(at == 0, hi, jnp.where(at == 1, mid, jnp.where(at == 2, low, 0.0)))
        tile = tile.astype(BF)
        for r in range(4):
            for k in range(4):
                if k != r:
                    w1[m, r, S + ADIM * k : S + ADIM * (k + 1), :] = (
                        tile if k == (r + 1) % 4 else jnp.zeros((ADIM, HID), BF)
                    )

    for d in NEAR:
        got = rows.at[x, zback(d)]
        remote(got, got, zs, zr.at[d], zpeer(d)).wait_recv()
        if d <= REACH or NZ - REACH < d:
            onward = REACH if d <= REACH else NZ - REACH
            remote(got, got, zs, zr.at[(d + onward) % NZ], zpeer(onward)).start()
        for j in range(1, NX):
            remote(got, got, xs, xr.at[j], xpeer(j)).start()

    own = rows[x].reshape(NZ, ROW)
    line_mean, line_std = own[:, 0:F], own[:, F : 2 * F]
    line_listed = eip[pl.ds(pl.multiple_of(x * NZ, NZ), NZ), :] // CD
    first_sum = jnp.zeros((NZ, F), F32)
    second_sum = jnp.zeros((NZ, F), F32)
    for j in range(NX):
        block = z * NX + xback(j)
        count = jnp.sum(jnp.where(line_listed == block, 1.0, 0.0), axis=1, keepdims=True)
        if j > 0:
            remote(elites.at[0], arrived.at[j], ns, nr.at[j], xpeer(j)).wait_recv()
        for s in range(CAP):
            drawn = (elites[x, s] if j == 0 else arrived[j, s]).astype(F32)
            a = jnp.clip(line_mean + line_std * drawn, -1.0, 1.0).astype(BF).astype(F32)
            a = jnp.where(count > float(s), a, 0.0)
            first_sum = first_sum + a
            second_sum = second_sum + a * a
    for k in range(4):
        cut = slice(128 * k, 128 * (k + 1))
        sums[pl.ds(k, NZ, stride=8), :] = first_sum[:, cut]
        sums[pl.ds(4 + k, NZ, stride=8), :] = second_sum[:, cut]

    for d in NEAR[::-1]:
        remote(
            sums.at[pl.ds(pl.multiple_of(lax.rem(z + d, NZ) * 8, 8), 8), :],
            parts.at[pl.ds(8 * d, 8), :],
            ss, sr, zpeer(d),
        ).start()

    for j in range(NX):
        k = xback(j)
        if j > 0:
            remote(rows.at[k], rows.at[k], xs, xr.at[j], xpeer(j)).wait_recv()
        line = rows[k].reshape(NZ, ROW)
        line_mean, line_std = line[:, 0:F], line[:, F : 2 * F]
        line_start = line[:, 2 * F : ROW]
        initial = -jnp.sum(line_start * line_start, axis=1, keepdims=True)
        for c in range(CD):
            m, h = c % M, c // M
            cut = slice(E * h + NZ * j, E * h + NZ * (j + 1))
            a = jnp.clip(line_mean + line_std * drawn_by(k, c), -1.0, 1.0).astype(BF)
            half = a * jnp.asarray(0.5, BF)
            for q in range(4):
                act[m, q, cut, :] = half[:, 128 * q : 128 * (q + 1)]
            a = a.astype(F32)
            asum[m, cut, :] = jnp.sum(a * a, axis=1, keepdims=True)
            states[m, cut, :] = line_start
            energy[m, cut, :] = initial

    pltpu.make_async_copy(wo_hbm, w2, load_sem.at[6]).wait()
    filled = w1.at[:, :, 0 : S + ADIM, :]
    pltpu.make_async_copy(filled, filled, load_sem.at[7]).wait()
    lane = lax.broadcasted_iota(jnp.int32, (2 * E, 128), 1)

    def squares(s):
        return jnp.sum(s * s, axis=1, keepdims=True)

    def step(q, r):
        left = []
        for m in range(M):
            s = states[m]
            e = squares(s)
            energy[m] = energy[m] + e
            n = (s * (0.5 * lax.rsqrt(e * (1.0 / S) + EPSILON))).astype(BF)
            at = ADIM * ((r + 1) % 4)
            ones = jnp.where((lane >= at) & (lane < at + 3), 0.5, 0.0).astype(BF)
            now = (lane >= ADIM * r) & (lane < ADIM * (r + 1))
            left.append((s, jnp.concatenate([n, jnp.where(now, act[m, q], ones)], axis=1)))
        halves = [
            jnp.dot(left[m][1], w1[m, r], preferred_element_type=F32) for m in range(M)
        ]
        for m in range(M):
            h = halves[m]
            hidden = (h + h * jnp.tanh(h)).astype(BF)
            states[m] = left[m][0] + jnp.dot(hidden, w2[m], preferred_element_type=F32)

    def quarter(q, carry):
        for r in range(4):
            step(q, r)
        return carry

    lax.fori_loop(0, 4, quarter, 0)

    out_lane = lax.broadcasted_iota(jnp.int32, (E, 128), 1)
    table = jnp.zeros((E, 128), F32)
    for c in range(CD):
        m, h = c % M, c // M
        cut = slice(E * h, E * (h + 1))
        e = energy[m, cut, :] + squares(states[m, cut, :])
        value = e * (-1.0 / (S * HOR)) - asum[m, cut, :] * (0.1 / (ADIM * HOR))
        table = jnp.where(out_lane == c, value, table)
    for j in range(NX):
        perm[pl.ds(xback(j), NZ, stride=NX), :] = table[NZ * j : NZ * (j + 1), :]
    ret_ref[...] = perm[...].T[0:CD, 0:E]

    others = parts.at[pl.ds(8, 8 * (NZ - 1)), :]
    remote(others, others, ss, sr, zpeer(1)).wait_recv()
    total = sums[pl.ds(pl.multiple_of(z * 8, 8), 8), :]
    for d in range(1, NZ):
        total = total + parts[8 * d : 8 * (d + 1), :]
    for k in range(4):
        cut = slice(128 * k, 128 * (k + 1))
        elite_mean = total[k : k + 1, :] * (1.0 / ELITE)
        elite_var = total[4 + k : 5 + k, :] * (1.0 / ELITE) - elite_mean * elite_mean
        nm_ref[:, cut] = ALPHA * mean_ref[:, cut] + (1.0 - ALPHA) * elite_mean
        nv_ref[:, cut] = ALPHA * var_ref[:, cut] + (1.0 - ALPHA) * elite_var

    remote(others, others, ss, sr, zpeer(1)).wait_send()
    sent = rows.at[0, pl.ds(0, NZ - 1)]
    remote(sent, sent, zs, zr.at[1], zpeer(1)).wait_send()
    sent = rows.at[pl.ds(0, NX - 1)]
    remote(sent, sent, xs, xr.at[1], xpeer(1)).wait_send()
    sent = arrived.at[pl.ds(1, NX - 1)]
    remote(sent, sent, ns, nr.at[1], xpeer(1)).wait_send()


def put_out(a, b, c, a_out, b_out, c_out, sem):
    copies = [
        pltpu.make_async_copy(src, dst, sem.at[i])
        for i, (src, dst) in enumerate(((a, a_out), (b, b_out), (c, c_out)))
    ]
    for copy in copies:
        copy.start()
    for copy in copies:
        copy.wait()


def per_device(*operands):
    vmem = pl.BlockSpec(memory_space=pltpu.VMEM)
    hbm = pl.BlockSpec(memory_space=pl.ANY)
    dma = pltpu.SemaphoreType.DMA
    shapes = (
            jax.ShapeDtypeStruct((CD, E), F32),
            jax.ShapeDtypeStruct((1, F), F32),
            jax.ShapeDtypeStruct((1, F), F32),
        )
    results = pl.pallas_call(
        kernel,
        out_shape=shapes,
        in_specs=[hbm] * 9,
        out_specs=(vmem, vmem, vmem),
        scratch_shapes=[
            pltpu.VMEM((1, F), F32),
            pltpu.VMEM((1, F), F32),
            pltpu.VMEM((1, S), F32),
            pltpu.VMEM((E, ELITE), jnp.int32),
            pltpu.VMEM((M, HID), F32),
            pltpu.VMEM((NX, NZ, 1, ROW), F32),
            pltpu.VMEM((E, CD, F), BF),
            pltpu.VMEM((4, E * CD, 128), F32),
            pltpu.VMEM((E, 128), jnp.int32),
            pltpu.VMEM((E, 128), jnp.int32),
            pltpu.VMEM((NX, CAP, NZ, F), BF),
            pltpu.VMEM((NX, CAP, NZ, F), BF),
            pltpu.VMEM((NZ * 8, 128), F32),
            pltpu.VMEM((NZ * 8, 128), F32),
            pltpu.VMEM((M, 4, 2 * S, HID), BF),
            pltpu.VMEM((M, HID, S), BF),
            pltpu.VMEM((M, 4, 2 * E, 128), BF),
            pltpu.VMEM((M, 2 * E, S), F32),
            pltpu.VMEM((M, 2 * E, 1), F32),
            pltpu.VMEM((M, 2 * E, 1), F32),
            pltpu.VMEM((128, 128), F32),
            dma((8,)), dma, dma((NZ,)), dma, dma((NX,)), dma, dma((NX,)), dma, dma,
        ],
        compiler_params=pltpu.CompilerParams(
            collective_id=0, has_side_effects=True, vmem_limit_bytes=24 * 2**20
        ),
    )(*(pltpu.with_memory_space_constraint(a, pltpu.HBM) for a in operands))
    returns, new_mean, new_var = pl.pallas_call(
        put_out,
        out_shape=shapes,
        in_specs=[vmem] * 3,
        out_specs=(hbm, hbm, hbm),
        scratch_shapes=[dma((3,))],
        compiler_params=pltpu.CompilerParams(vmem_limit_bytes=24 * 2**20),
    )(*results)
    return returns.T, new_mean, new_var


def solution(mesh):
    both = P(("env", "cand"), None)
    in_specs = (both, both, both, P("env", "cand", None), P("env", None), P(), P(), P(), P())
    return jax.shard_map(
        per_device, mesh=mesh, in_specs=in_specs, out_specs=(P("env", "cand"), both, both),
        check_vma=False,
    )
```

time: 38.6 us -> 34.8 us (0.902)
  Pallas kernels: 37.8 us -> 34 us
    pallas_call x1, Pallas kernels: 36.5 us -> 33.4 us  [per_device(): pl.pallas_call(kernel, out_shape=shapes, in_specs=[hbm] * 9, out_specs=(v...]
    pallas_call x1, Pallas kernels: 1.29 us -> 0.63 us  [per_device(): pl.pallas_call(put_out, out_shape=shapes, in_specs=[vmem] * 3, out_specs=...]
where the time goes in v3:
time: 34.8 us; the launch traced here: 34.7 us
  Pallas kernels  34 us (98%)
  between operations  0.64 us (2%)
    pallas_call x1, Pallas kernels, per_device(): pl.pallas_call(kernel, out_shape=shapes, in_specs=[hbm] * 9, out_specs=(v...  33.4 us

profile of v3, /device:TPU:24, one launch (start us, length us, event | category | flops | bytes accessed | tf_op | source)
XLA Modules:
  0.0 34.7 jit_solution(8591922533389266554)
XLA Ops:
  0.6 33.4 %shard_map.112 = (f32[8,64]{1,0:T(8,128)S(1)}, f32[1,512]{1,0:T(1,128)S(1)}, f32[1,512]{1,0:T(1,128)S(1)}) custom-call(f32[1,512]{1,0:T(1,128)} %mean_hbm.1, f32[1,512]{1,0:T(1,128)} %var_hbm.1, f32[1,128]{1,0:T(1,128)} %start_hbm.1, bf16[64,8,512]{2,1,0:T(8,128)(2,1)} %noise_hbm.1, s32[64,64]{1,0:T(8,128)} %elite_hbm.1, bf16[4,128,512]{2,1,0:T(8,128)(2,1)} %ws_hbm.1, ...), custom_call_target="tpu_custom_call" | custom-call | tf_op jit(solution)/shard_map/pallas_call | solution.py:284
  34.0 0.6 %shard_map.113 = (f32[8,64]{1,0:T(8,128)}, f32[1,512]{1,0:T(1,128)}, f32[1,512]{1,0:T(1,128)}) custom-call(f32[8,64]{1,0:T(8,128)S(1)} %get-tuple-element.9.a, f32[1,512]{1,0:T(1,128)S(1)} %get-tuple-element.10.b, f32[1,512]{1,0:T(1,128)S(1)} %get-tuple-element.11.c), custom_call_target="tpu_custom_call" | custom-call | tf_op jit(solution)/shard_map/pallas_call | solution.py:317

commit v4 on v3

--- a/solution.py
+++ b/solution.py
@@ -25,18 +25,22 @@
 def kernel(
     mean_hbm, var_hbm, start_hbm, noise_hbm, elite_hbm, ws_hbm, wa_hbm, bias_hbm, wo_hbm,
     ret_ref, nm_ref, nv_ref,
-    mean_ref, var_ref, start_ref, elite_ref, bias_ref, rows, noise_v, noise_f, wide, eip, elites, arrived, sums, parts, w1, w2, act, states, energy,
+    mean_ref, var_ref, start_ref, elite_ref, bias_ref, rows, guests, noise_v, noise_f, noise_c, wide, eip, elites, arrived, sums, parts, w1, w2, act, states, energy,
     asum, perm,
-    load_sem, zs, zr, xs, xr, ns, nr, ss, sr,
+    load_sem, gs, gr, zs, zr, xs, xr, ns, nr, ss, sr,
 ):
     me = lax.axis_index("cand")
     z, x = lax.div(me, NX), lax.rem(me, NX)
 
-    def zpeer(d):
-        return {"cand": lax.rem(me + NX * d, E)}
-
-    def xpeer(j):
-        return {"cand": z * NX + lax.rem(x + j, NX)}
+    env = lax.axis_index("env")
+    core = lax.rem(env, 2)
+    relays_two, is_guest = core == 1, core == 0
+
+    def zpeer(d, over=0):
+        return {"cand": lax.rem(me + NX * d, E), "env": env + over}
+
+    def xpeer(j, over=0):
+        return {"cand": z * NX + lax.rem(x + j, NX), "env": env + over}
 
     def zback(d):
         return lax.rem(z + NZ - d, NZ)
@@ -60,10 +64,23 @@
     for c in small[:3]:
         c.start()
     barrier = pltpu.get_barrier_semaphore()
-    for d in DIRECT[::-1]:
-        pl.semaphore_signal(barrier, inc=1, device_id=zpeer(d), device_id_type=pl.DeviceIdType.MESH)
+
+    def greet(peer):
+        pl.semaphore_signal(barrier, inc=1, device_id=peer, device_id_type=pl.DeviceIdType.MESH)
+
+    @pl.when(relays_two)
+    def _():
+        for d in DIRECT[::-1]:
+            greet(zpeer(d, -1))
+            greet(zpeer(d))
+
+    @pl.when(is_guest)
+    def _():
+        for j in range(NX):
+            greet(xpeer(j, 1))
+
     for j in range(1, NX):
-        pl.semaphore_signal(barrier, inc=1, device_id=xpeer(j), device_id_type=pl.DeviceIdType.MESH)
+        greet(xpeer(j))
     for c in small[3:]:
         c.start()
 
@@ -73,11 +90,20 @@
     rows[x, z, :, F : 2 * F] = jnp.sqrt(var_ref[...])
     rows[x, z, :, 2 * F : ROW] = start_ref[...]
 
-    pl.semaphore_wait(barrier, len(DIRECT) + NX - 1)
+    pl.semaphore_wait(barrier, len(DIRECT) + NX - 1 + NX * core)
 
     mine = rows.at[x, z]
-    for d in DIRECT[::-1]:
-        remote(mine, mine, zs, zr.at[d], zpeer(d)).start()
+
+    @pl.when(relays_two)
+    def _():
+        for d in DIRECT[::-1]:
+            remote(mine, mine, zs, zr.at[d], zpeer(d)).start()
+
+    @pl.when(is_guest)
+    def _():
+        for d in DIRECT[::-1]:
+            remote(mine, guests.at[z], zs, gr.at[d], zpeer(d, 1)).start()
+
     for j in range(1, NX):
         remote(mine, mine, xs, xr.at[j], xpeer(j)).start()
 
@@ -98,10 +124,6 @@
     for q in range(4):
         part = noise_v[:, :, 128 * q : 128 * (q + 1)]
         noise_f[q] = part.astype(F32).reshape(E * CD, 128)
-
-    def drawn_by(k, c):
-        at = pl.ds(k * CD + c, NZ, stride=NX * CD)
-        return jnp.concatenate([noise_f[q, at, :] for q in range(4)], axis=1)
 
     for k in range(NX):
         listed = eip[NZ * k : NZ * (k + 1), :]
@@ -110,7 +132,9 @@
         for c in range(CD):
             hit = jnp.where(listed == me * CD + c, 1.0, 0.0)
             chosen = jnp.sum(hit, axis=1, keepdims=True)
-            drawn = drawn_by(k, c)
+            at = pl.ds(k * CD + c, NZ, stride=NX * CD)
+            drawn = jnp.concatenate([noise_f[q, at, :] for q in range(4)], axis=1)
+            noise_c[k, c] = drawn
             place = jnp.where(chosen > 0.5, before, -1.0)
             for s in range(min(c + 1, CAP)):
                 slots[s] = jnp.where(place == float(s), drawn, slots[s])
@@ -137,14 +161,30 @@
                         tile if k == (r + 1) % 4 else jnp.zeros((ADIM, HID), BF)
                     )
 
-    for d in NEAR:
-        got = rows.at[x, zback(d)]
-        remote(got, got, zs, zr.at[d], zpeer(d)).wait_recv()
-        if d <= REACH or NZ - REACH < d:
+    @pl.when(relays_two)
+    def _():
+        for d in NEAR:
+            near = d <= REACH or NZ - REACH < d
             onward = REACH if d <= REACH else NZ - REACH
-            remote(got, got, zs, zr.at[(d + onward) % NZ], zpeer(onward)).start()
-        for j in range(1, NX):
-            remote(got, got, xs, xr.at[j], xpeer(j)).start()
+            far = (d + onward) % NZ
+            guest, seat = guests.at[zback(d)], rows.at[x, zback(d)]
+            remote(guest, guest, gs.at[1], gr.at[d], zpeer(d)).wait_recv()
+            if near:
+                remote(guest, guest, gs.at[1], gr.at[far], zpeer(onward)).start()
+            for j in (2, 1, 3):
+                remote(guest, seat, gs.at[0], xr.at[j], xpeer(j, -1)).start()
+            remote(guest, seat, gs.at[1], zr.at[d], xpeer(0, -1)).start()
+            remote(seat, seat, zs, zr.at[d], zpeer(d)).wait_recv()
+            if near:
+                remote(seat, seat, zs, zr.at[far], zpeer(onward)).start()
+            for j in (2, 1, 3):
+                remote(seat, seat, xs, xr.at[j], xpeer(j)).start()
+
+    @pl.when(is_guest)
+    def _():
+        for d in NEAR:
+            seat = rows.at[x, zback(d)]
+            remote(seat, seat, zs, zr.at[d], zpeer(d)).wait_recv()
 
     own = rows[x].reshape(NZ, ROW)
     line_mean, line_std = own[:, 0:F], own[:, F : 2 * F]
@@ -185,7 +225,7 @@
         for c in range(CD):
             m, h = c % M, c // M
             cut = slice(E * h + NZ * j, E * h + NZ * (j + 1))
-            a = jnp.clip(line_mean + line_std * drawn_by(k, c), -1.0, 1.0).astype(BF)
+            a = jnp.clip(line_mean + line_std * noise_c[k, c], -1.0, 1.0).astype(BF)
             half = a * jnp.asarray(0.5, BF)
             for q in range(4):
                 act[m, q, cut, :] = half[:, 128 * q : 128 * (q + 1)]
@@ -253,10 +293,25 @@
         nv_ref[:, cut] = ALPHA * var_ref[:, cut] + (1.0 - ALPHA) * elite_var
 
     remote(others, others, ss, sr, zpeer(1)).wait_send()
-    sent = rows.at[0, pl.ds(0, NZ - 1)]
-    remote(sent, sent, zs, zr.at[1], zpeer(1)).wait_send()
-    sent = rows.at[pl.ds(0, NX - 1)]
-    remote(sent, sent, xs, xr.at[1], xpeer(1)).wait_send()
+
+    @pl.when(relays_two)
+    def _():
+        near_and_far = rows.at[0, pl.ds(0, NZ - 1)]
+        remote(near_and_far, near_and_far, zs, zr.at[1], zpeer(1)).wait_send()
+        sideways = rows.at[pl.ds(0, NX - 1)]
+        remote(sideways, sideways, xs, xr.at[1], xpeer(1)).wait_send()
+        guests_sideways = rows.at[pl.ds(0, NX - 1), pl.ds(0, NZ - 1)]
+        remote(guests_sideways, guests_sideways, gs.at[0], xr.at[1], xpeer(1)).wait_send()
+        guests_other = rows.at[pl.ds(0, 2), pl.ds(0, (2 * NZ + REACH * 2 - 2 - NZ) // 2)]
+        remote(guests_other, guests_other, gs.at[1], xr.at[1], xpeer(1)).wait_send()
+
+    @pl.when(is_guest)
+    def _():
+        near = rows.at[0, pl.ds(0, len(DIRECT))]
+        remote(near, near, zs, zr.at[1], zpeer(1)).wait_send()
+        sideways = rows.at[0, pl.ds(0, NX - 1)]
+        remote(sideways, sideways, xs, xr.at[1], xpeer(1)).wait_send()
+
     sent = arrived.at[pl.ds(1, NX - 1)]
     remote(sent, sent, ns, nr.at[1], xpeer(1)).wait_send()
 
@@ -293,8 +348,10 @@
             pltpu.VMEM((E, ELITE), jnp.int32),
             pltpu.VMEM((M, HID), F32),
             pltpu.VMEM((NX, NZ, 1, ROW), F32),
+            pltpu.VMEM((NZ, 1, ROW), F32),
             pltpu.VMEM((E, CD, F), BF),
             pltpu.VMEM((4, E * CD, 128), F32),
+            pltpu.VMEM((NX, CD, NZ, F), F32),
             pltpu.VMEM((E, 128), jnp.int32),
             pltpu.VMEM((E, 128), jnp.int32),
             pltpu.VMEM((NX, CAP, NZ, F), BF),
@@ -308,7 +365,7 @@
             pltpu.VMEM((M, 2 * E, 1), F32),
             pltpu.VMEM((M, 2 * E, 1), F32),
             pltpu.VMEM((128, 128), F32),
-            dma((8,)), dma, dma((NZ,)), dma, dma((NX,)), dma, dma((NX,)), dma, dma,
+            dma((8,)), dma((2,)), dma((NZ,)), dma, dma((NZ,)), dma, dma((NX,)), dma, dma((NX,)), dma, dma,
         ],
         compiler_params=pltpu.CompilerParams(
             collective_id=0, has_side_effects=True, vmem_limit_bytes=24 * 2**20

time: 34.8 us -> 33.6 us (0.966)
  the two profiles are of different devices: /device:TPU:24 before, /device:TPU:1 now
where the time goes in v4:
time: 33.6 us; the launch traced here: 33.5 us
  Pallas kernels  32.8 us (98%)
  between operations  0.64 us (2%)
    pallas_call x1, Pallas kernels, per_device(): pl.pallas_call(kernel, out_shape=shapes, in_specs=[hbm] * 9, out_specs=(v...  32.2 us

profile of v4, /device:TPU:1, one launch (start us, length us, event | category | flops | bytes accessed | tf_op | source)
XLA Modules:
  0.0 33.5 jit_solution(2342287950996233897)
XLA Ops:
  0.6 32.2 %shard_map.112 = (f32[8,64]{1,0:T(8,128)S(1)}, f32[1,512]{1,0:T(1,128)S(1)}, f32[1,512]{1,0:T(1,128)S(1)}) custom-call(f32[1,512]{1,0:T(1,128)} %mean_hbm.1, f32[1,512]{1,0:T(1,128)} %var_hbm.1, f32[1,128]{1,0:T(1,128)} %start_hbm.1, bf16[64,8,512]{2,1,0:T(8,128)(2,1)} %noise_hbm.1, s32[64,64]{1,0:T(8,128)} %elite_hbm.1, bf16[4,128,512]{2,1,0:T(8,128)(2,1)} %ws_hbm.1, ...), custom_call_target="tpu_custom_call" | custom-call | tf_op jit(solution)/shard_map/pallas_call | solution.py:339
  32.8 0.6 %shard_map.113 = (f32[8,64]{1,0:T(8,128)}, f32[1,512]{1,0:T(1,128)}, f32[1,512]{1,0:T(1,128)}) custom-call(f32[8,64]{1,0:T(8,128)S(1)} %get-tuple-element.9.a, f32[1,512]{1,0:T(1,128)S(1)} %get-tuple-element.10.b, f32[1,512]{1,0:T(1,128)S(1)} %get-tuple-element.11.c), custom_call_target="tpu_custom_call" | custom-call | tf_op jit(solution)/shard_map/pallas_call | solution.py:374

commit v5 on v4

--- a/solution.py
+++ b/solution.py
@@ -168,17 +168,17 @@
             onward = REACH if d <= REACH else NZ - REACH
             far = (d + onward) % NZ
             guest, seat = guests.at[zback(d)], rows.at[x, zback(d)]
+            remote(seat, seat, zs, zr.at[d], zpeer(d)).wait_recv()
+            if near:
+                remote(seat, seat, zs, zr.at[far], zpeer(onward)).start()
+            for j in (2, 1, 3):
+                remote(seat, seat, xs, xr.at[j], xpeer(j)).start()
             remote(guest, guest, gs.at[1], gr.at[d], zpeer(d)).wait_recv()
             if near:
                 remote(guest, guest, gs.at[1], gr.at[far], zpeer(onward)).start()
             for j in (2, 1, 3):
                 remote(guest, seat, gs.at[0], xr.at[j], xpeer(j, -1)).start()
             remote(guest, seat, gs.at[1], zr.at[d], xpeer(0, -1)).start()
-            remote(seat, seat, zs, zr.at[d], zpeer(d)).wait_recv()
-            if near:
-                remote(seat, seat, zs, zr.at[far], zpeer(onward)).start()
-            for j in (2, 1, 3):
-                remote(seat, seat, xs, xr.at[j], xpeer(j)).start()
 
     @pl.when(is_guest)
     def _():

time: 33.6 us -> 33.3 us (level)
  no operation moved by 1% of the time
where the time goes in v5:
time: 33.3 us; the launch traced here: 33.2 us
  Pallas kernels  32.6 us (98%)
  between operations  0.64 us (2%)
    pallas_call x1, Pallas kernels, per_device(): pl.pallas_call(kernel, out_shape=shapes, in_specs=[hbm] * 9, out_specs=(v...  31.9 us

profile of v5, /device:TPU:1, one launch (start us, length us, event | category | flops | bytes accessed | tf_op | source)
XLA Modules:
  0.0 33.2 jit_solution(4974188434121141502)
XLA Ops:
  0.6 31.9 %shard_map.112 = (f32[8,64]{1,0:T(8,128)S(1)}, f32[1,512]{1,0:T(1,128)S(1)}, f32[1,512]{1,0:T(1,128)S(1)}) custom-call(f32[1,512]{1,0:T(1,128)} %mean_hbm.1, f32[1,512]{1,0:T(1,128)} %var_hbm.1, f32[1,128]{1,0:T(1,128)} %start_hbm.1, bf16[64,8,512]{2,1,0:T(8,128)(2,1)} %noise_hbm.1, s32[64,64]{1,0:T(8,128)} %elite_hbm.1, bf16[4,128,512]{2,1,0:T(8,128)(2,1)} %ws_hbm.1, ...), custom_call_target="tpu_custom_call" | custom-call | tf_op jit(solution)/shard_map/pallas_call | solution.py:339
  32.6 0.6 %shard_map.113 = (f32[8,64]{1,0:T(8,128)}, f32[1,512]{1,0:T(1,128)}, f32[1,512]{1,0:T(1,128)}) custom-call(f32[8,64]{1,0:T(8,128)S(1)} %get-tuple-element.9.a, f32[1,512]{1,0:T(1,128)S(1)} %get-tuple-element.10.b, f32[1,512]{1,0:T(1,128)S(1)} %get-tuple-element.11.c), custom_call_target="tpu_custom_call" | custom-call | tf_op jit(solution)/shard_map/pallas_call | solution.py:374
